TPU v7x, 128 devices: a whole 4x4x4 slice. The times are simulated.
128 devices in a mesh: head: 16 (over z, y), batch: 8 (over x, core).
Axes of the slice: x: 4, y: 4, z: 4, core: 2. Of those that a mesh axis runs over, the one named last changes fastest.
Arguments:
- incoming_hidden_stream: bfloat16 [1024, 4096], P('batch'), may hold values from -6 to 6
- reception_projection: bfloat16 [4096, 4096], P(None, 'head'), may hold values from -0.09375 to 0.09375
- address_projection: bfloat16 [4096, 4096], P(None, 'head'), may hold values from -0.09375 to 0.09375
- payload_projection: bfloat16 [4096, 4096], P(None, 'head'), may hold values from -0.09375 to 0.09375
- sigmoid_filter_matrix: bfloat16 [4096, 4096], P(None, 'head'), may hold values from -0.09375 to 0.09375
- forgetting_speed: float32 [1024, 4096], P('batch', 'head'), may hold values from 0.01 to 1.5
- adaptation_step_size: float32 [1024, 4096], P('batch', 'head'), may hold values from 0 to 1
- diagonal_boost: float32 [4096], P('head'), may hold values from -0.6 to 0.6
- subspace_standardize_scale: float32 [4096], P('head'), may hold values from 0.5 to 2
- recurrent_memory_matrix: float32 [128, 64, 64, 64], P('batch', 'head'), may hold values from -6 to 6
- emission_projection: bfloat16 [4096, 4096], P('head'), may hold values from -0.09375 to 0.09375
- closing_standardize_scale: float32 [4096], replicated, may hold values from 0.7 to 2
- lexicon_projection: bfloat16 [4096, 65536], P(None, ('head', 'batch')), may hold values from -32 to 32
- proposed_tokens_list: int32 [128, 8], P('batch'), may hold values from 0 to 65535
- threshold_milli_nats: int32 [128, 8], P('batch'), may hold values from -22000 to -10001
Outputs:
- new_state: float32 [128, 64, 64, 64], P('batch', 'head')
- margin: float32 [128, 8], P('batch')
- accept: float32 [128, 8], P('batch')
All inputs are finite; a program needn't handle non-finite values.
Results may differ from a plain program's by a relative error of at most 0.0017.
Values may be sent and summed in bfloat16 or wider, within the bound.
A program may use at most 128 MiB of HBM per device.

v0:
```python
import math
import jax
import jax.numpy as jnp
from jax import lax
from jax.sharding import Mesh
from jax.sharding import PartitionSpec as P

HEAD = ("head_0", "head_1")
HEAD_BATCH = ("head_0", "head_1", "batch")


def in_blocks(x, dim, size):
    before, after = (x.shape[:dim], x.shape[dim + 1 :])
    return jnp.moveaxis(x.reshape(*before, size, -1, *after), dim, 0)


def sent_and_summed(x, axis, dim):
    size = lax.axis_size(axis)
    parts = lax.all_to_all(in_blocks(x, dim, size), axis, 0, 0, tiled=True)
    return jnp.sum(parts, axis=0)


def by_axis(x, axes):
    for axis in axes:
        x = lax.psum(x, axis)
    return x


def joined_along(parts, dim):
    parts = jnp.moveaxis(parts, 0, dim)
    shape = parts.shape
    return parts.reshape(*shape[:dim], shape[dim] * shape[dim + 1], *shape[dim + 2 :])


def sent_to_all(x, axis):
    copies = jnp.broadcast_to(x, (lax.axis_size(axis), *x.shape))
    return lax.all_to_all(copies, axis, split_axis=0, concat_axis=0, tiled=True)


def gathered_copies(x, axis, dim):
    return joined_along(sent_to_all(x, axis), dim)


def gathered_once(x, axis):
    leaves = jax.tree.leaves(x)
    sequence = sorted(range(len(leaves)), key=lambda k: -leaves[k].size)
    width = (1, *leaves[sequence[0]].shape)[-1]
    lines = [
        jnp.pad(leaves[k].reshape(-1), (0, -leaves[k].size % width)).reshape(-1, width)
        for k in sequence
    ]
    both, at, found = (sent_to_all(jnp.concatenate(lines), axis), 0, {})
    for k, line in zip(sequence, lines):
        share = both[:, at : at + len(line)].reshape(len(both), -1)
        found[k] = share[:, : leaves[k].size].reshape(-1, *leaves[k].shape)
        at += len(line)
    numbers = iter(range(len(leaves)))
    return jax.tree.map(lambda _: found[next(numbers)], x)


def combined_pairwise(pieces, combine):
    while len(jax.tree.leaves(pieces)[0]) > 1:
        pieces = jax.vmap(combine)(
            *(jax.tree.map(lambda part: part[side::2], pieces) for side in (0, 1))
        )
    return jax.tree.map(lambda part: part[0], pieces)


def combined_all(x, axis, combine):
    pieces = gathered_once(x, axis)
    return combined_pairwise(pieces, combine)


def gathered_by_type(x, axis):
    leaves, found = (jax.tree.leaves(x), {})
    for initial, a in enumerate(leaves):
        if initial not in found:
            alike = [k for k, b in enumerate(leaves) if b.dtype == a.dtype]
            got = (
                gathered_once([leaves[k] for k in alike], axis)
                if len(alike) > 1
                else [sent_to_all(a, axis)]
            )
            for k, b in zip(alike, got):
                found[k] = b
    numbers = iter(range(len(leaves)))
    return jax.tree.map(lambda _: found[next(numbers)], x)


def merged(x, axis, combine):
    pieces = gathered_by_type(x, axis)
    return combined_pairwise(pieces, combine)


def advance(start, reception_vectors, address_vectors, payload_vectors, decay, rate):
    unit = (
        address_vectors
        * lax.rsqrt(jnp.mean(address_vectors * address_vectors, -1, keepdims=True) + 1e-06)
        / math.sqrt(address_vectors.shape[-1])
    )
    inputs = tuple(
        (
            jnp.moveaxis(item, 1, 0)
            for item in (reception_vectors, address_vectors, payload_vectors, decay, unit, rate)
        )
    )

    def step(current, pieces):
        recept_now, keys_now, values_now, decay_now, unit_now, rate_now = pieces
        recall = jnp.einsum("bhij,bhj->bhi", current, unit_now, precision=lax.Precision.HIGHEST)
        current = (
            current * decay_now[:, :, None, :]
            - recall[:, :, :, None] * (unit_now * rate_now)[:, :, None, :]
            + values_now[:, :, :, None] * keys_now[:, :, None, :]
        )
        output = jnp.einsum("bhij,bhj->bhi", current, recept_now, precision=lax.Precision.HIGHEST)
        return (current, output)

    final, outputs = lax.scan(step, start, inputs)
    return (final, jnp.moveaxis(outputs, 0, 1))


def combine_stats(first, second):
    top = jnp.maximum(first[0], second[0])
    summed = first[1] * jnp.exp(first[0] - top) + second[1] * jnp.exp(second[0] - top)
    return (top, summed, first[2] + second[2])


def local_stats(logits, ids_flat, offset):
    peak = jnp.max(logits, -1)
    total = jnp.sum(jnp.exp(logits - peak[:, None]), -1)
    column = lax.broadcasted_iota(jnp.int32, logits.shape, 1)
    target = jnp.sum(jnp.where(column == (ids_flat - offset)[:, None], logits, 0.0), -1)
    return (peak, total, target)


def shards(
    incoming_hidden_stream,
    reception_projection,
    address_projection,
    payload_projection,
    sigmoid_filter_matrix,
    forgetting_speed,
    adaptation_step_size,
    diagonal_boost,
    subspace_standardize_scale,
    recurrent_memory_matrix,
    emission_projection,
    closing_standardize_scale,
    lexicon_projection,
    proposed_tokens_list,
    threshold_milli_nats,
):
    seq_dev, draft_len = proposed_tokens_list.shape
    lanes_on_shard, subspace_size = (
        recurrent_memory_matrix.shape[1],
        recurrent_memory_matrix.shape[2],
    )
    tok_dev = seq_dev * draft_len
    width = incoming_hidden_stream.shape[1]
    shape4 = (seq_dev, draft_len, lanes_on_shard, subspace_size)
    reception_vectors = jnp.dot(
        incoming_hidden_stream, reception_projection, preferred_element_type=jnp.float32
    ).reshape(shape4)
    address_vectors = jnp.dot(
        incoming_hidden_stream, address_projection, preferred_element_type=jnp.float32
    ).reshape(shape4)
    payload_vectors = jnp.dot(
        incoming_hidden_stream, payload_projection, preferred_element_type=jnp.float32
    ).reshape(shape4)
    gate = jnp.dot(
        incoming_hidden_stream, sigmoid_filter_matrix, preferred_element_type=jnp.float32
    )
    decay = jnp.exp(-forgetting_speed).reshape(shape4)
    rate = adaptation_step_size.reshape(shape4)
    new_state, wkv = advance(
        recurrent_memory_matrix, reception_vectors, address_vectors, payload_vectors, decay, rate
    )
    center = wkv - jnp.mean(wkv, -1, keepdims=True)
    interpolated_embedding = (
        center
        * lax.rsqrt(jnp.mean(center * center, -1, keepdims=True) + 1e-05)
        * subspace_standardize_scale.reshape(lanes_on_shard, subspace_size)
    )
    interpolated_embedding = (
        interpolated_embedding
        + jnp.sum(
            reception_vectors
            * address_vectors
            * diagonal_boost.reshape(lanes_on_shard, subspace_size),
            -1,
            keepdims=True,
        )
        * payload_vectors
    )
    gated = (
        interpolated_embedding.reshape(tok_dev, lanes_on_shard * subspace_size)
        * jax.nn.sigmoid(gate)
    ).astype(jnp.bfloat16)
    partial_out = jnp.dot(gated, emission_projection, preferred_element_type=jnp.float32)
    share = sent_and_summed(partial_out, HEAD, 1)
    cols = share.shape[1]
    begin = lax.axis_index(HEAD) * cols
    residual = (
        lax.dynamic_slice_in_dim(incoming_hidden_stream, begin, cols, 1).astype(jnp.float32) + share
    )
    moment_one, moment_two = (
        by_axis(jnp.sum(residual, -1), HEAD),
        by_axis(jnp.sum(residual * residual, -1), HEAD),
    )
    mean_row = moment_one / width
    variance = moment_two / width - mean_row * mean_row
    gain_part = lax.dynamic_slice_in_dim(closing_standardize_scale, begin, cols, 0)
    normed_part = (
        (residual - mean_row[:, None]) * lax.rsqrt(variance + 1e-05)[:, None] * gain_part
    ).astype(jnp.bfloat16)
    normed = gathered_copies(normed_part, HEAD, 1)
    every, every_ids = (
        lax.all_gather(normed, "batch", axis=0, tiled=True),
        lax.all_gather(proposed_tokens_list, "batch", axis=0, tiled=True),
    )
    logits = jnp.dot(every, lexicon_projection, preferred_element_type=jnp.float32)
    vcols = lexicon_projection.shape[1]
    offset = (lax.axis_index(HEAD) * lax.axis_size("batch") + lax.axis_index("batch")) * vcols
    peak, total, target = local_stats(logits, every_ids.reshape(-1), offset)
    peak, total, target = combined_all((peak, total, target), "batch", combine_stats)
    row_begin = lax.axis_index("batch") * tok_dev
    peak = lax.dynamic_slice_in_dim(peak, row_begin, tok_dev, 0)
    total = lax.dynamic_slice_in_dim(total, row_begin, tok_dev, 0)
    target = lax.dynamic_slice_in_dim(target, row_begin, tok_dev, 0)
    top, summed, target = merged((peak, total, target), HEAD, combine_stats)
    logprob = target - (top + jnp.log(summed))
    margin = logprob.reshape(seq_dev, draft_len) - threshold_milli_nats.astype(jnp.float32) / 1000.0
    accept = jnp.cumprod(jax.nn.sigmoid(margin * 0.5), axis=1)
    return (new_state, margin, accept)


def solution(mesh):
    split = Mesh(mesh.devices.reshape(4, 4, mesh.shape["batch"]), ("head_0", "head_1", "batch"))
    return jax.shard_map(
        shards,
        mesh=split,
        in_specs=(
            P("batch", None),
            P(None, HEAD),
            P(None, HEAD),
            P(None, HEAD),
            P(None, HEAD),
            P("batch", HEAD),
            P("batch", HEAD),
            P(HEAD),
            P(HEAD),
            P("batch", HEAD, None, None),
            P(HEAD, None),
            P(),
            P(None, HEAD_BATCH),
            P("batch", None),
            P("batch", None),
        ),
        out_specs=(P("batch", HEAD, None, None), P("batch", None), P("batch", None)),
        check_vma=False,
    )
```

profile of v0, /device:TPU:0, one launch (start us, length us, event | category | flops | bytes accessed | tf_op | source)
XLA Modules:
  0.0 318.9 jit_solution(11417522193714851282)
XLA Ops:
  29.0 105.4 %while.12 = (s32[]{:T(128)}, f32[16,4,64,64]{3,2,1,0:T(8,128)}, f32[8,16,4,64]{3,2,1,0:T(4,128)S(1)}, f32[8,16,4,64]{3,2,0,1:T(4,128)}, f32[8,16,4,64]{3,2,1,0:T...) while((s32[]{:T(128)}, f32[16,4,64,64]{3,2,1,0:T(8,128)}, ...), condition=%wide.region_2.3_spmd, body=%wide.region_1.2_spmd.sunk | while | flops 7606274 | bytes 13009081 | solution.py:119
  31.5 4.9 %fusion.54 = f32[16,4,1,64]{3,2,1,0:T(1,128)S(1)} fusion(f32[16,4,64,1]{2,3,1,0:T(1,128)S(1)} %bitcast.118, f32[16,4,64,64]{3,2,1,0:T(8,128)} %get-tuple-element.245), kind=kOutput, calls=%fused_computation.79.clone.1 | convolution fusion | flops 3145728 | bytes 1081344 | tf_op jit(solution)/shard_map/while/body/eval_jaxpr/bhij,bhj->bhi/dot_general | solution.py:110
  44.7 4.9 %fusion.54 = f32[16,4,1,64]{3,2,1,0:T(1,128)S(1)} fusion(f32[16,4,64,1]{2,3,1,0:T(1,128)S(1)} %bitcast.118, f32[16,4,64,64]{3,2,1,0:T(8,128)} %get-tuple-element.245), kind=kOutput, calls=%fused_computation.79.clone.1 | convolution fusion | flops 3145728 | bytes 1081344 | tf_op jit(solution)/shard_map/while/body/eval_jaxpr/bhij,bhj->bhi/dot_general | solution.py:110
  52.0 3.3 %fusion.55 = f32[16,4,1,64]{3,2,1,0:T(1,128)S(1)} fusion(f32[16,4,64,64]{3,2,1,0:T(8,128)S(1)} %multiply_add_fusion.8, f32[16,4,64,1]{2,3,1,0:T(1,128)S(1)} %bitcast.117), kind=kOutput, calls=%fused_computation.80.clone.1 | convolution fusion | flops 3145728 | bytes 1081344 | tf_op jit(solution)/shard_map/while/body/eval_jaxpr/bhij,bhj->bhi/dot_general | solution.py:116
  57.9 4.9 %fusion.54 = f32[16,4,1,64]{3,2,1,0:T(1,128)S(1)} fusion(f32[16,4,64,1]{2,3,1,0:T(1,128)S(1)} %bitcast.118, f32[16,4,64,64]{3,2,1,0:T(8,128)} %get-tuple-element.245), kind=kOutput, calls=%fused_computation.79.clone.1 | convolution fusion | flops 3145728 | bytes 1081344 | tf_op jit(solution)/shard_map/while/body/eval_jaxpr/bhij,bhj->bhi/dot_general | solution.py:110
  71.0 4.9 %fusion.54 = f32[16,4,1,64]{3,2,1,0:T(1,128)S(1)} fusion(f32[16,4,64,1]{2,3,1,0:T(1,128)S(1)} %bitcast.118, f32[16,4,64,64]{3,2,1,0:T(8,128)} %get-tuple-element.245), kind=kOutput, calls=%fused_computation.79.clone.1 | convolution fusion | flops 3145728 | bytes 1081344 | tf_op jit(solution)/shard_map/while/body/eval_jaxpr/bhij,bhj->bhi/dot_general | solution.py:110
  78.3 3.3 %fusion.55 = f32[16,4,1,64]{3,2,1,0:T(1,128)S(1)} fusion(f32[16,4,64,64]{3,2,1,0:T(8,128)S(1)} %multiply_add_fusion.8, f32[16,4,64,1]{2,3,1,0:T(1,128)S(1)} %bitcast.117), kind=kOutput, calls=%fused_computation.80.clone.1 | convolution fusion | flops 3145728 | bytes 1081344 | tf_op jit(solution)/shard_map/while/body/eval_jaxpr/bhij,bhj->bhi/dot_general | solution.py:116
  84.2 4.9 %fusion.54 = f32[16,4,1,64]{3,2,1,0:T(1,128)S(1)} fusion(f32[16,4,64,1]{2,3,1,0:T(1,128)S(1)} %bitcast.118, f32[16,4,64,64]{3,2,1,0:T(8,128)} %get-tuple-element.245), kind=kOutput, calls=%fused_computation.79.clone.1 | convolution fusion | flops 3145728 | bytes 1081344 | tf_op jit(solution)/shard_map/while/body/eval_jaxpr/bhij,bhj->bhi/dot_general | solution.py:110
  97.4 4.9 %fusion.54 = f32[16,4,1,64]{3,2,1,0:T(1,128)S(1)} fusion(f32[16,4,64,1]{2,3,1,0:T(1,128)S(1)} %bitcast.118, f32[16,4,64,64]{3,2,1,0:T(8,128)} %get-tuple-element.245), kind=kOutput, calls=%fused_computation.79.clone.1 | convolution fusion | flops 3145728 | bytes 1081344 | tf_op jit(solution)/shard_map/while/body/eval_jaxpr/bhij,bhj->bhi/dot_general | solution.py:110
  110.6 4.9 %fusion.54 = f32[16,4,1,64]{3,2,1,0:T(1,128)S(1)} fusion(f32[16,4,64,1]{2,3,1,0:T(1,128)S(1)} %bitcast.118, f32[16,4,64,64]{3,2,1,0:T(8,128)} %get-tuple-element.245), kind=kOutput, calls=%fused_computation.79.clone.1 | convolution fusion | flops 3145728 | bytes 1081344 | tf_op jit(solution)/shard_map/while/body/eval_jaxpr/bhij,bhj->bhi/dot_general | solution.py:110
  123.8 4.9 %fusion.54 = f32[16,4,1,64]{3,2,1,0:T(1,128)S(1)} fusion(f32[16,4,64,1]{2,3,1,0:T(1,128)S(1)} %bitcast.118, f32[16,4,64,64]{3,2,1,0:T(8,128)} %get-tuple-element.245), kind=kOutput, calls=%fused_computation.79.clone.1 | convolution fusion | flops 3145728 | bytes 1081344 | tf_op jit(solution)/shard_map/while/body/eval_jaxpr/bhij,bhj->bhi/dot_general | solution.py:110
  139.9 4.2 %fusion.5 = f32[128,4096]{1,0:T(8,128)} fusion(bf16[256,4096]{1,0:T(8,128)(2,1)S(1)} %copy-done, f32[128,256]{1,0:T(8,128)S(1)} %reshape.129, bf16[128,4096]{1,0:T(8,128)(2,1)S(1)} %copy-done.3, bf16[4096,256]{1,0:T(8,128)(2,1)} %param.21), kind=kOutput, calls=%fused_computation.18 | convolution fusion | flops 537034752 | bytes 7471104 | tf_op jit(solution)/shard_map/dot_general | solution.py:200
  147.3 8.2 %all-to-all-start = ((f32[16,128,256]{2,1,0:T(8,128)}), f32[16,128,256]{2,1,0:T(8,128)}, u32[]{:S(2)}, u32[]{:S(2)}) async-start(f32[16,128,256]{2,1,0:T(8,128)} %bitcast.113), calls=%async_computation | async-start | bytes 4194304 | tf_op jit(solution)/shard_map/all_to_all | solution.py:19
  156.4 31.0 %all-to-all-done = f32[16,128,256]{2,1,0:T(8,128)} async-done(((f32[16,128,256]{2,1,0:T(8,128)}), f32[16,128,256]{2,1,0:T(8,128)}, u32[]{:S(2)}, u32[]{:S(2)}) %all-to-all-start) | async-done | bytes 2097184 | tf_op jit(solution)/shard_map/all_to_all | solution.py:19
  189.2 9.5 %all-reduce.1 = (f32[128]{0:T(128)S(1)}, f32[128]{0:T(128)S(1)}) all-reduce(f32[128]{0:T(128)S(1)} %get-tuple-element.107, f32[128]{0:T(128)S(1)} %get-tuple-element.106), channel_id=1, replica_groups=mesh['head_0'=4,'head_1'=4,'batch'=8] {'head_0'}, use_global_device_ids=true, to_apply=%region_11.12 | all-reduce | flops 256 | bytes 2048 | tf_op jit(solution)/shard_map/psum | solution.py:25
  198.7 7.7 %all-reduce = (f32[128]{0:T(128)S(1)}, f32[128]{0:T(128)S(1)}) all-reduce(f32[128]{0:T(128)S(1)} %get-tuple-element.130, f32[128]{0:T(128)S(1)} %get-tuple-element.131), channel_id=1, replica_groups=mesh['head_0'=4,'head_1'=4,'batch'=8] {'head_1'}, use_global_device_ids=true, to_apply=%region_12.13 | all-reduce | flops 256 | bytes 2048 | tf_op jit(solution)/shard_map/psum | solution.py:25
  206.9 16.6 %all_to_all.20 = bf16[16,128,256]{1,2,0:T(8,128)(2,1)} all-to-all(bf16[16,128,256]{1,2,0:T(8,128)(2,1)S(1)} %broadcast_in_dim.21), channel_id=1, replica_groups=mesh['head_0'=4,'head_1'=4,'batch'=8] {'head_0','head_1'}, dimensions={0} | all-to-all | bytes 2097152 | tf_op jit(solution)/shard_map/all_to_all | solution.py:37
  223.5 13.3 %all-gather = s32[8,16,8]{1,2,0:T(8,128)S(1)} all-gather(s32[1,16,8]{1,2,0:T(8,128)S(1)} %bitcast.136), channel_id=1, replica_groups=mesh['head_0'=4,'head_1'=4,'batch'=8] {'batch'}, dimensions={0}, use_global_device_ids=true | all-gather | bytes 4608 | tf_op jit(solution)/shard_map/all_gather | solution.py:220
  237.0 37.6 %all-gather.3.cloned.1.call-done = bf16[1024,4096]{0,1:T(8,128)(2,1)} async-done(((bf16[128,4096]{0,1:T(8,128)(2,1)}), bf16[1024,4096]{0,1:T(8,128)(2,1)}) %all-gather.3.cloned.1.call-update) | async-done | bytes 8388624 | tf_op jit(solution)/shard_map/all_gather | solution.py:219
  274.6 8.3 %fusion.23 = (f32[1024]{0:T(1024)S(1)}, f32[1024,512]{0,1:T(8,128)S(1)}) fusion(bf16[1024,4096]{0,1:T(8,128)(2,1)} %all-gather.3.cloned.1.call-done, bf16[4096,512]{1,0:T(8,128)(2,1)} %param.29), kind=kOutput, calls=%fused_computation.78 | convolution fusion | flops 4295490560 | bytes 14684160 | tf_op jit(solution)/shard_map/dot_general | solution.py:222
  284.1 4.0 %all-to-all-start.2 = ((f32[8,3,1024]{2,1,0:T(4,128)}), f32[8,3,1024]{2,1,0:T(4,128)S(1)}, u32[]{:S(2)}, u32[]{:S(2)}) async-start(f32[8,3,1024]{2,1,0:T(4,128)} %broadcast_in_dim.23), calls=%async_computation.2 | async-start | bytes 262144 | tf_op jit(solution)/shard_map/all_to_all | solution.py:37
  288.1 6.1 %all-to-all-done.2 = f32[8,3,1024]{2,1,0:T(4,128)S(1)} async-done(((f32[8,3,1024]{2,1,0:T(4,128)}), f32[8,3,1024]{2,1,0:T(4,128)S(1)}, u32[]{:S(2)}, u32[]{:S(2)}) %all-to-all-start.2) | async-done | bytes 98336 | tf_op jit(solution)/shard_map/all_to_all | solution.py:37
  295.4 6.9 %all-to-all-start.3 = ((f32[16,3,128]{2,1,0:T(4,128)}), f32[16,3,128]{2,1,0:T(4,128)S(1)}, u32[]{:S(2)}, u32[]{:S(2)}) async-start(f32[16,3,128]{2,1,0:T(4,128)} %broadcast_in_dim.25), calls=%async_computation.3 | async-start | bytes 65536 | tf_op jit(solution)/shard_map/all_to_all | solution.py:37
  302.5 7.5 %all-to-all-done.3 = f32[16,3,128]{2,1,0:T(4,128)S(1)} async-done(((f32[16,3,128]{2,1,0:T(4,128)}), f32[16,3,128]{2,1,0:T(4,128)S(1)}, u32[]{:S(2)}, u32[]{:S(2)}) %all-to-all-start.3) | async-done | bytes 24608 | tf_op jit(solution)/shard_map/all_to_all | solution.py:37
  (206 shorter events, 97.0 us)
Async XLA Ops:
  7.2 132.8 %copy-start = (bf16[256,4096]{1,0:T(8,128)(2,1)S(1)}, bf16[256,4096]{1,0:T(8,128)(2,1)}, u32[]{:S(2)}) copy-start(bf16[256,4096]{1,0:T(8,128)(2,1)} %param.27) | copy-start | bytes 6291460
  7.2 5.1 %copy-start.3 = (bf16[128,4096]{1,0:T(8,128)(2,1)S(1)}, bf16[128,4096]{1,0:T(8,128)(2,1)}, u32[]{:S(2)}) copy-start(bf16[128,4096]{1,0:T(8,128)(2,1)} %param.17) | copy-start | bytes 3145732
  14.3 3.7 %copy-start.7 = (f32[256]{0:T(256)S(1)}, f32[256]{0:T(256)}, u32[]{:S(2)}) copy-start(f32[256]{0:T(256)} %param.24) | copy-start | bytes 3076
  29.0 105.5 %copy-start.4 = (f32[16,8,4]{2,1,0:T(8,128)S(1)}, f32[16,8,4]{2,1,0:T(8,128)}, u32[]{:S(2)}) copy-start(f32[16,8,4]{2,1,0:T(8,128)} %get-tuple-element.108) | copy-start | bytes 6148
  29.0 106.1 %copy-start.8 = (f32[256]{0:T(256)S(1)}, f32[256]{0:T(256)}, u32[]{:S(2)}) copy-start(f32[256]{0:T(256)} %param.25) | copy-start | bytes 3076
  29.0 8.2 %copy-start.1 = (f32[16,4,64,64]{3,2,1,0:T(8,128)S(1)}, f32[16,4,64,64]{3,2,1,0:T(8,128)}, u32[]{:S(2)}) copy-start(f32[16,4,64,64]{3,2,1,0:T(8,128)} %get-tuple-element.245) | copy-start | bytes 3145732 | tf_op jit(solution)/shard_map/while
  38.8 3.4 %copy-start.2 = (f32[16,4,64,64]{3,2,1,0:T(8,128)}, f32[16,4,64,64]{3,2,1,0:T(8,128)S(1)}, u32[]{:S(2)}) copy-start(f32[16,4,64,64]{3,2,1,0:T(8,128)S(1)} %multiply_add_fusion.8) | copy-start | bytes 3145732 | tf_op jit(solution)/shard_map/while
  42.2 8.2 %copy-start.1 = (f32[16,4,64,64]{3,2,1,0:T(8,128)S(1)}, f32[16,4,64,64]{3,2,1,0:T(8,128)}, u32[]{:S(2)}) copy-start(f32[16,4,64,64]{3,2,1,0:T(8,128)} %get-tuple-element.245) | copy-start | bytes 3145732 | tf_op jit(solution)/shard_map/while
  51.9 3.4 %copy-start.2 = (f32[16,4,64,64]{3,2,1,0:T(8,128)}, f32[16,4,64,64]{3,2,1,0:T(8,128)S(1)}, u32[]{:S(2)}) copy-start(f32[16,4,64,64]{3,2,1,0:T(8,128)S(1)} %multiply_add_fusion.8) | copy-start | bytes 3145732 | tf_op jit(solution)/shard_map/while
  55.3 8.2 %copy-start.1 = (f32[16,4,64,64]{3,2,1,0:T(8,128)S(1)}, f32[16,4,64,64]{3,2,1,0:T(8,128)}, u32[]{:S(2)}) copy-start(f32[16,4,64,64]{3,2,1,0:T(8,128)} %get-tuple-element.245) | copy-start | bytes 3145732 | tf_op jit(solution)/shard_map/while
  68.5 8.2 %copy-start.1 = (f32[16,4,64,64]{3,2,1,0:T(8,128)S(1)}, f32[16,4,64,64]{3,2,1,0:T(8,128)}, u32[]{:S(2)}) copy-start(f32[16,4,64,64]{3,2,1,0:T(8,128)} %get-tuple-element.245) | copy-start | bytes 3145732 | tf_op jit(solution)/shard_map/while
  78.3 3.4 %copy-start.2 = (f32[16,4,64,64]{3,2,1,0:T(8,128)}, f32[16,4,64,64]{3,2,1,0:T(8,128)S(1)}, u32[]{:S(2)}) copy-start(f32[16,4,64,64]{3,2,1,0:T(8,128)S(1)} %multiply_add_fusion.8) | copy-start | bytes 3145732 | tf_op jit(solution)/shard_map/while
  81.7 8.2 %copy-start.1 = (f32[16,4,64,64]{3,2,1,0:T(8,128)S(1)}, f32[16,4,64,64]{3,2,1,0:T(8,128)}, u32[]{:S(2)}) copy-start(f32[16,4,64,64]{3,2,1,0:T(8,128)} %get-tuple-element.245) | copy-start | bytes 3145732 | tf_op jit(solution)/shard_map/while
  94.9 8.2 %copy-start.1 = (f32[16,4,64,64]{3,2,1,0:T(8,128)S(1)}, f32[16,4,64,64]{3,2,1,0:T(8,128)}, u32[]{:S(2)}) copy-start(f32[16,4,64,64]{3,2,1,0:T(8,128)} %get-tuple-element.245) | copy-start | bytes 3145732 | tf_op jit(solution)/shard_map/while
  104.7 3.4 %copy-start.2 = (f32[16,4,64,64]{3,2,1,0:T(8,128)}, f32[16,4,64,64]{3,2,1,0:T(8,128)S(1)}, u32[]{:S(2)}) copy-start(f32[16,4,64,64]{3,2,1,0:T(8,128)S(1)} %multiply_add_fusion.8) | copy-start | bytes 3145732 | tf_op jit(solution)/shard_map/while
  108.1 8.2 %copy-start.1 = (f32[16,4,64,64]{3,2,1,0:T(8,128)S(1)}, f32[16,4,64,64]{3,2,1,0:T(8,128)}, u32[]{:S(2)}) copy-start(f32[16,4,64,64]{3,2,1,0:T(8,128)} %get-tuple-element.245) | copy-start | bytes 3145732 | tf_op jit(solution)/shard_map/while
  121.3 8.2 %copy-start.1 = (f32[16,4,64,64]{3,2,1,0:T(8,128)S(1)}, f32[16,4,64,64]{3,2,1,0:T(8,128)}, u32[]{:S(2)}) copy-start(f32[16,4,64,64]{3,2,1,0:T(8,128)} %get-tuple-element.245) | copy-start | bytes 3145732 | tf_op jit(solution)/shard_map/while
  131.0 3.4 %copy-start.2 = (f32[16,4,64,64]{3,2,1,0:T(8,128)}, f32[16,4,64,64]{3,2,1,0:T(8,128)S(1)}, u32[]{:S(2)}) copy-start(f32[16,4,64,64]{3,2,1,0:T(8,128)S(1)} %multiply_add_fusion.8) | copy-start | bytes 3145732 | tf_op jit(solution)/shard_map/while
  147.3 40.1 %all-to-all-start = ((f32[16,128,256]{2,1,0:T(8,128)}), f32[16,128,256]{2,1,0:T(8,128)}, u32[]{:S(2)}, u32[]{:S(2)}) async-start(f32[16,128,256]{2,1,0:T(8,128)} %bitcast.113), calls=%async_computation | async-start | bytes 4194304 | tf_op jit(solution)/shard_map/all_to_all | solution.py:19
  155.5 119.1 %all-gather.3.cloned.1.call-start = ((), (), s32[]{:S(2)}) async-start(), calls=%async_computation.4 | async-start | bytes 9437184 | tf_op jit(solution)/shard_map/all_gather | solution.py:219
  206.7 16.9 %copy-start.5 = (s32[16,8]{0,1:T(8,128)S(1)}, s32[16,8]{0,1:T(8,128)}, u32[]{:S(2)}) copy-start(s32[16,8]{0,1:T(8,128)} %param.30) | copy-start | bytes 1540
  282.9 19.5 %copy-start.6 = (s32[16,8]{0,1:T(8,128)S(1)}, s32[16,8]{0,1:T(8,128)}, u32[]{:S(2)}) copy-start(s32[16,8]{0,1:T(8,128)} %param.31) | copy-start | bytes 1540
  284.1 10.1 %all-to-all-start.2 = ((f32[8,3,1024]{2,1,0:T(4,128)}), f32[8,3,1024]{2,1,0:T(4,128)S(1)}, u32[]{:S(2)}, u32[]{:S(2)}) async-start(f32[8,3,1024]{2,1,0:T(4,128)} %broadcast_in_dim.23), calls=%async_computation.2 | async-start | bytes 262144 | tf_op jit(solution)/shard_map/all_to_all | solution.py:37
  295.4 14.6 %all-to-all-start.3 = ((f32[16,3,128]{2,1,0:T(4,128)}), f32[16,3,128]{2,1,0:T(4,128)S(1)}, u32[]{:S(2)}, u32[]{:S(2)}) async-start(f32[16,3,128]{2,1,0:T(4,128)} %broadcast_in_dim.25), calls=%async_computation.3 | async-start | bytes 65536 | tf_op jit(solution)/shard_map/all_to_all | solution.py:37
  (3 other events, 10.1 us)
Sparse Core Ops, SparseCore 0:
  223.6 50.9 all-gather.2
where the time goes:
time: 321 us; the launch traced here: 319 us
  matrix products  84.9 us (26%)
  waiting for transfers between devices  82.3 us (26%)
  blocking collectives  47.1 us (15%)
  local copies, waits for them, and re-layouts  41.7 us (13%)
  other arithmetic  29.1 us (9%)
  starting transfers between devices  19.2 us (6%)
  between operations  14.4 us (4%)
    dot_general x8, matrix products, step(): jnp.einsum('bhij,bhj->bhi', current, unit_now, precision=lax.Precision.HI...  39.5 us
    all_gather x1, waiting for transfers between devices, shards(): lax.all_gather(normed, 'batch', axis=0, tiled=True)  37.6 us
    all_to_all x1, waiting for transfers between devices, sent_and_summed(): parts = lax.all_to_all(in_blocks(x, dim, size), axis, 0, 0, tiled=True)  31 us
    dot_general x8, matrix products, step(): jnp.einsum('bhij,bhj->bhi', current, recept_now, precision=lax.Precision....  26.8 us
    psum x2, blocking collectives, by_axis(): x = lax.psum(x, axis)  17.2 us
    all_to_all x1, blocking collectives, sent_to_all(): return lax.all_to_all(copies, axis, split_axis=0, concat_axis=0, tiled=True)  16.6 us
    all_to_all x2, waiting for transfers between devices, sent_to_all(): return lax.all_to_all(copies, axis, split_axis=0, concat_axis=0, tiled=True)  13.6 us
    all_gather x1, blocking collectives, shards(): lax.all_gather(proposed_tokens_list, 'batch', axis=0, tiled=True)  13.3 us
  transfers between devices with their start and end apart: 4, of which 4 were waited for; matrix products, arithmetic and copies ran while one was open for 0% of the time, Pallas kernels for 0%

commit v1 on v0

--- a/solution.py
+++ b/solution.py
@@ -7,6 +7,19 @@
 
 HEAD = ("head_0", "head_1")
 HEAD_BATCH = ("head_0", "head_1", "batch")
+
+
+def ring_gather(x, axis, dim):
+    ways = lax.axis_size(axis)
+    up = [(d, (d + 1) % ways) for d in range(ways)]
+    down = [(d, (d - 1) % ways) for d in range(ways)]
+    earlier, later = ([x], [x])
+    for _ in range(ways // 2):
+        earlier.append(lax.ppermute(earlier[-1], axis, up))
+    for _ in range((ways - 1) // 2):
+        later.append(lax.ppermute(later[-1], axis, down))
+    line = jnp.concatenate([*earlier[::-1], *later[1:]], axis=dim)
+    return jnp.roll(line, (lax.axis_index(axis) - ways // 2) * x.shape[dim], axis=dim)
 
 
 def in_blocks(x, dim, size):
@@ -216,7 +229,7 @@
     ).astype(jnp.bfloat16)
     normed = gathered_copies(normed_part, HEAD, 1)
     every, every_ids = (
-        lax.all_gather(normed, "batch", axis=0, tiled=True),
+        ring_gather(normed, "batch", 0),
         lax.all_gather(proposed_tokens_list, "batch", axis=0, tiled=True),
     )
     logits = jnp.dot(every, lexicon_projection, preferred_element_type=jnp.float32)

time: 321 us -> 340 us (1.059)
  local copies, waits for them, and re-layouts: 41.7 us -> 57.4 us
  between operations: 14.4 us -> 1.22 us
  blocking collectives: 47.1 us -> 55.1 us
  waiting for transfers between devices: 82.3 us -> 90.1 us
  starting transfers between devices: 19.2 us -> 22.9 us
  matrix products: 84.9 us -> 81.3 us
    ppermute x0 -> x7, waiting for transfers between devices: none -> 45.5 us  [the longest x4 40.4 us: ring_gather(): earlier.append(lax.ppermute(earlier[-1], axis, up))]
    all_gather x1 -> x0, waiting for transfers between devices: 37.6 us -> none  [shards(): lax.all_gather(normed, 'batch', axis=0, tiled=True)]
    unnamed x21 -> x46, local copies, waits for them, and re-layouts: 4.79 us -> 20.2 us
    all_gather x1, blocking collectives: 13.3 us -> 21.4 us  [shards(): lax.all_gather(proposed_tokens_list, 'batch', axis=0, tiled=True)]
    ppermute x0 -> x7, starting transfers between devices: none -> 6.92 us  [the longest x3 6.9 us: ring_gather(): later.append(lax.ppermute(later[-1], axis, down))]
    dot_general x1, matrix products: 8.27 us -> 4.66 us  [shards(): jnp.dot(every, lexicon_projection, preferred_element_type=jnp.float32)]
  transfers between devices with their start and end apart: 4 -> 10, of which waited for: 4 -> 7; matrix products, arithmetic and copies ran while one was open for 0% -> 3% of each run, Pallas kernels for 0% -> 0%
where the time goes in v1:
time: 340 us; the launch traced here: 338 us
  waiting for transfers between devices  90.1 us (26%)
  matrix products  81.3 us (24%)
  local copies, waits for them, and re-layouts  57.4 us (17%)
  blocking collectives  55.1 us (16%)
  other arithmetic  29.1 us (9%)
  starting transfers between devices  22.9 us (7%)
    ppermute x4, waiting for transfers between devices, ring_gather(): earlier.append(lax.ppermute(earlier[-1], axis, up))  40.4 us
    dot_general x8, matrix products, step(): jnp.einsum('bhij,bhj->bhi', current, unit_now, precision=lax.Precision.HI...  39.5 us
    all_to_all x1, waiting for transfers between devices, sent_and_summed(): parts = lax.all_to_all(in_blocks(x, dim, size), axis, 0, 0, tiled=True)  31.1 us
    dot_general x8, matrix products, step(): jnp.einsum('bhij,bhj->bhi', current, recept_now, precision=lax.Precision....  26.8 us
    all_gather x1, blocking collectives, shards(): lax.all_gather(proposed_tokens_list, 'batch', axis=0, tiled=True)  21.4 us
    unnamed x46, local copies, waits for them, and re-layouts  20.2 us
    psum x2, blocking collectives, by_axis(): x = lax.psum(x, axis)  17.2 us
    all_to_all x1, blocking collectives, sent_to_all(): return lax.all_to_all(copies, axis, split_axis=0, concat_axis=0, tiled=True)  16.5 us
  transfers between devices with their start and end apart: 10, of which 7 were waited for; matrix products, arithmetic and copies ran while one was open for 3% of the time, Pallas kernels for 0%

profile of v1, /device:TPU:0, one launch (start us, length us, event | category | flops | bytes accessed | tf_op | source)
XLA Modules:
  0.0 337.5 jit_solution(17819999361865850470)
XLA Ops:
  22.4 105.4 %while.12 = (s32[]{:T(128)}, f32[16,4,64,64]{3,2,1,0:T(8,128)}, f32[8,16,4,64]{3,2,1,0:T(4,128)S(1)}, f32[8,16,4,64]{3,2,0,1:T(4,128)}, f32[8,16,4,64]{3,2,1,0:T...) while((s32[]{:T(128)}, f32[16,4,64,64]{3,2,1,0:T(8,128)}, ...), condition=%wide.region_2.3_spmd, body=%wide.region_1.2_spmd.sunk | while | flops 7606274 | bytes 13009081 | solution.py:132
  24.9 4.9 %fusion.56 = f32[16,4,1,64]{3,2,1,0:T(1,128)S(1)} fusion(f32[16,4,64,1]{2,3,1,0:T(1,128)S(1)} %bitcast.120, f32[16,4,64,64]{3,2,1,0:T(8,128)} %get-tuple-element.245), kind=kOutput, calls=%fused_computation.98.clone.1 | convolution fusion | flops 3145728 | bytes 1081344 | tf_op jit(solution)/shard_map/while/body/eval_jaxpr/bhij,bhj->bhi/dot_general | solution.py:123
  38.1 4.9 %fusion.56 = f32[16,4,1,64]{3,2,1,0:T(1,128)S(1)} fusion(f32[16,4,64,1]{2,3,1,0:T(1,128)S(1)} %bitcast.120, f32[16,4,64,64]{3,2,1,0:T(8,128)} %get-tuple-element.245), kind=kOutput, calls=%fused_computation.98.clone.1 | convolution fusion | flops 3145728 | bytes 1081344 | tf_op jit(solution)/shard_map/while/body/eval_jaxpr/bhij,bhj->bhi/dot_general | solution.py:123
  51.3 4.9 %fusion.56 = f32[16,4,1,64]{3,2,1,0:T(1,128)S(1)} fusion(f32[16,4,64,1]{2,3,1,0:T(1,128)S(1)} %bitcast.120, f32[16,4,64,64]{3,2,1,0:T(8,128)} %get-tuple-element.245), kind=kOutput, calls=%fused_computation.98.clone.1 | convolution fusion | flops 3145728 | bytes 1081344 | tf_op jit(solution)/shard_map/while/body/eval_jaxpr/bhij,bhj->bhi/dot_general | solution.py:123
  64.5 4.9 %fusion.56 = f32[16,4,1,64]{3,2,1,0:T(1,128)S(1)} fusion(f32[16,4,64,1]{2,3,1,0:T(1,128)S(1)} %bitcast.120, f32[16,4,64,64]{3,2,1,0:T(8,128)} %get-tuple-element.245), kind=kOutput, calls=%fused_computation.98.clone.1 | convolution fusion | flops 3145728 | bytes 1081344 | tf_op jit(solution)/shard_map/while/body/eval_jaxpr/bhij,bhj->bhi/dot_general | solution.py:123
  77.7 4.9 %fusion.56 = f32[16,4,1,64]{3,2,1,0:T(1,128)S(1)} fusion(f32[16,4,64,1]{2,3,1,0:T(1,128)S(1)} %bitcast.120, f32[16,4,64,64]{3,2,1,0:T(8,128)} %get-tuple-element.245), kind=kOutput, calls=%fused_computation.98.clone.1 | convolution fusion | flops 3145728 | bytes 1081344 | tf_op jit(solution)/shard_map/while/body/eval_jaxpr/bhij,bhj->bhi/dot_general | solution.py:123
  90.8 4.9 %fusion.56 = f32[16,4,1,64]{3,2,1,0:T(1,128)S(1)} fusion(f32[16,4,64,1]{2,3,1,0:T(1,128)S(1)} %bitcast.120, f32[16,4,64,64]{3,2,1,0:T(8,128)} %get-tuple-element.245), kind=kOutput, calls=%fused_computation.98.clone.1 | convolution fusion | flops 3145728 | bytes 1081344 | tf_op jit(solution)/shard_map/while/body/eval_jaxpr/bhij,bhj->bhi/dot_general | solution.py:123
  104.0 4.9 %fusion.56 = f32[16,4,1,64]{3,2,1,0:T(1,128)S(1)} fusion(f32[16,4,64,1]{2,3,1,0:T(1,128)S(1)} %bitcast.120, f32[16,4,64,64]{3,2,1,0:T(8,128)} %get-tuple-element.245), kind=kOutput, calls=%fused_computation.98.clone.1 | convolution fusion | flops 3145728 | bytes 1081344 | tf_op jit(solution)/shard_map/while/body/eval_jaxpr/bhij,bhj->bhi/dot_general | solution.py:123
  117.2 4.9 %fusion.56 = f32[16,4,1,64]{3,2,1,0:T(1,128)S(1)} fusion(f32[16,4,64,1]{2,3,1,0:T(1,128)S(1)} %bitcast.120, f32[16,4,64,64]{3,2,1,0:T(8,128)} %get-tuple-element.245), kind=kOutput, calls=%fused_computation.98.clone.1 | convolution fusion | flops 3145728 | bytes 1081344 | tf_op jit(solution)/shard_map/while/body/eval_jaxpr/bhij,bhj->bhi/dot_general | solution.py:123
  133.3 4.2 %fusion.7 = f32[128,4096]{1,0:T(8,128)} fusion(bf16[256,4096]{1,0:T(8,128)(2,1)S(1)} %copy-done, f32[128,256]{1,0:T(8,128)S(1)} %reshape.129, bf16[128,4096]{1,0:T(8,128)(2,1)S(1)} %copy-done.3, bf16[4096,256]{1,0:T(8,128)(2,1)} %param.21), kind=kOutput, calls=%fused_computation.20 | convolution fusion | flops 537034752 | bytes 7471104 | tf_op jit(solution)/shard_map/dot_general | solution.py:213
  140.7 8.2 %all-to-all-start = ((f32[16,128,256]{2,1,0:T(8,128)}), f32[16,128,256]{2,1,0:T(8,128)}, u32[]{:S(2)}, u32[]{:S(2)}) async-start(f32[16,128,256]{2,1,0:T(8,128)} %bitcast.116), calls=%async_computation | async-start | bytes 4194304 | tf_op jit(solution)/shard_map/all_to_all | solution.py:32
  149.7 31.1 %all-to-all-done = f32[16,128,256]{2,1,0:T(8,128)} async-done(((f32[16,128,256]{2,1,0:T(8,128)}), f32[16,128,256]{2,1,0:T(8,128)}, u32[]{:S(2)}, u32[]{:S(2)}) %all-to-all-start) | async-done | bytes 2097184 | tf_op jit(solution)/shard_map/all_to_all | solution.py:32
  182.7 9.5 %all-reduce.1 = (f32[128]{0:T(128)S(1)}, f32[128]{0:T(128)S(1)}) all-reduce(f32[128]{0:T(128)S(1)} %get-tuple-element.107, f32[128]{0:T(128)S(1)} %get-tuple-element.106), channel_id=1, replica_groups=mesh['head_0'=4,'head_1'=4,'batch'=8] {'head_0'}, use_global_device_ids=true, to_apply=%region_11.12 | all-reduce | flops 256 | bytes 2048 | tf_op jit(solution)/shard_map/psum | solution.py:38
  192.1 7.7 %all-reduce = (f32[128]{0:T(128)S(1)}, f32[128]{0:T(128)S(1)}) all-reduce(f32[128]{0:T(128)S(1)} %get-tuple-element.130, f32[128]{0:T(128)S(1)} %get-tuple-element.131), channel_id=1, replica_groups=mesh['head_0'=4,'head_1'=4,'batch'=8] {'head_1'}, use_global_device_ids=true, to_apply=%region_12.13 | all-reduce | flops 256 | bytes 2048 | tf_op jit(solution)/shard_map/psum | solution.py:38
  200.3 16.5 %all_to_all.20 = bf16[16,128,256]{1,2,0:T(8,128)(2,1)S(1)} all-to-all(bf16[16,128,256]{1,2,0:T(8,128)(2,1)S(1)} %broadcast_in_dim.21), channel_id=1, replica_groups=mesh['head_0'=4,'head_1'=4,'batch'=8] {'head_0','head_1'}, dimensions={0} | all-to-all | bytes 2097152 | tf_op jit(solution)/shard_map/all_to_all | solution.py:50
  216.8 15.4 %collective-permute-done = bf16[128,4096]{0,1:T(8,128)(2,1)S(1)} collective-permute-done((bf16[128,4096]{0,1:T(8,128)(2,1)S(1)}, bf16[128,4096]{0,1:T(8,128)(2,1)S(1)}, u32[]{:S(2)}, u32[]{:S(2)}) %collective-permute-start) | collective-permute-done | bytes 1048608 | tf_op jit(solution)/shard_map/ppermute | solution.py:18
  235.2 12.5 %collective-permute-done.1 = bf16[128,4096]{0,1:T(8,128)(2,1)S(1)} collective-permute-done((bf16[128,4096]{0,1:T(8,128)(2,1)S(1)}, bf16[128,4096]{0,1:T(8,128)(2,1)S(1)}, u32[]{:S(2)}, u32[]{:S(2)}) %collective-permute-start.1) | collective-permute-done | bytes 1048608 | tf_op jit(solution)/shard_map/ppermute | solution.py:18
  250.8 12.5 %collective-permute-done.2 = bf16[128,4096]{0,1:T(8,128)(2,1)} collective-permute-done((bf16[128,4096]{0,1:T(8,128)(2,1)S(1)}, bf16[128,4096]{0,1:T(8,128)(2,1)}, u32[]{:S(2)}, u32[]{:S(2)}) %collective-permute-start.2) | collective-permute-done | bytes 1048608 | tf_op jit(solution)/shard_map/ppermute | solution.py:18
  263.2 21.4 %all-gather = s32[8,16,8]{1,2,0:T(8,128)S(1)} all-gather(s32[1,16,8]{1,2,0:T(8,128)S(1)} %bitcast.138), channel_id=1, replica_groups=mesh['head_0'=4,'head_1'=4,'batch'=8] {'batch'}, dimensions={0}, use_global_device_ids=true | all-gather | bytes 4608 | tf_op jit(solution)/shard_map/all_gather | solution.py:233
  293.3 5.1 %collective-permute-done.6 = bf16[128,4096]{0,1:T(8,128)(2,1)S(1)} collective-permute-done((bf16[128,4096]{0,1:T(8,128)(2,1)}, bf16[128,4096]{0,1:T(8,128)(2,1)S(1)}, u32[]{:S(2)}, u32[]{:S(2)}) %collective-permute-start.6) | collective-permute-done | bytes 1048608 | tf_op jit(solution)/shard_map/ppermute | solution.py:20
  306.8 4.7 %fusion.26 = (f32[1024]{0:T(1024)S(1)}, f32[1024,512]{0,1:T(8,128)S(1)}) fusion(bf16[4096,512]{1,0:T(8,128)(2,1)S(1)} %copy-done.13, bf16[2048,4096]{0,1:T(8,128)(2,1)S(1)} %constant_dynamic-update-slice_fusion.1, s32[]{:T(128)S(6)} %select_n.28), kind=kOutput, calls=%fused_computation.97 | convolution fusion | flops 4295490560 | bytes 14684164 | tf_op jit(solution)/shard_map/dot_general | solution.py:235
  312.8 4.3 %all-to-all-start.2 = ((f32[8,3,1024]{2,1,0:T(4,128)}), f32[8,3,1024]{2,1,0:T(4,128)S(1)}, u32[]{:S(2)}, u32[]{:S(2)}) async-start(f32[8,3,1024]{2,1,0:T(4,128)} %broadcast_in_dim.23), calls=%async_computation.2 | async-start | bytes 262144 | tf_op jit(solution)/shard_map/all_to_all | solution.py:50
  317.1 6.1 %all-to-all-done.2 = f32[8,3,1024]{2,1,0:T(4,128)S(1)} async-done(((f32[8,3,1024]{2,1,0:T(4,128)}), f32[8,3,1024]{2,1,0:T(4,128)S(1)}, u32[]{:S(2)}, u32[]{:S(2)}) %all-to-all-start.2) | async-done | bytes 98336 | tf_op jit(solution)/shard_map/all_to_all | solution.py:50
  328.0 7.5 %all-to-all-done.3 = f32[16,3,128]{2,1,0:T(4,128)S(1)} async-done(((f32[16,3,128]{2,1,0:T(4,128)}), f32[16,3,128]{2,1,0:T(4,128)S(1)}, u32[]{:S(2)}, u32[]{:S(2)}) %all-to-all-start.3) | async-done | bytes 24608 | tf_op jit(solution)/shard_map/all_to_all | solution.py:50
  (243 shorter events, 129.7 us)
Async XLA Ops:
  0.6 132.7 %copy-start = (bf16[256,4096]{1,0:T(8,128)(2,1)S(1)}, bf16[256,4096]{1,0:T(8,128)(2,1)}, u32[]{:S(2)}) copy-start(bf16[256,4096]{1,0:T(8,128)(2,1)} %param.27) | copy-start | bytes 6291460
  22.4 105.5 %copy-start.8 = (f32[16,8,4]{2,1,0:T(8,128)S(1)}, f32[16,8,4]{2,1,0:T(8,128)}, u32[]{:S(2)}) copy-start(f32[16,8,4]{2,1,0:T(8,128)} %get-tuple-element.108) | copy-start | bytes 6148
  22.4 106.1 %copy-start.12 = (f32[256]{0:T(256)S(1)}, f32[256]{0:T(256)}, u32[]{:S(2)}) copy-start(f32[256]{0:T(256)} %param.25) | copy-start | bytes 3076
  22.4 8.2 %copy-start.1 = (f32[16,4,64,64]{3,2,1,0:T(8,128)S(1)}, f32[16,4,64,64]{3,2,1,0:T(8,128)}, u32[]{:S(2)}) copy-start(f32[16,4,64,64]{3,2,1,0:T(8,128)} %get-tuple-element.245) | copy-start | bytes 3145732 | tf_op jit(solution)/shard_map/while
  35.6 8.2 %copy-start.1 = (f32[16,4,64,64]{3,2,1,0:T(8,128)S(1)}, f32[16,4,64,64]{3,2,1,0:T(8,128)}, u32[]{:S(2)}) copy-start(f32[16,4,64,64]{3,2,1,0:T(8,128)} %get-tuple-element.245) | copy-start | bytes 3145732 | tf_op jit(solution)/shard_map/while
  48.8 8.2 %copy-start.1 = (f32[16,4,64,64]{3,2,1,0:T(8,128)S(1)}, f32[16,4,64,64]{3,2,1,0:T(8,128)}, u32[]{:S(2)}) copy-start(f32[16,4,64,64]{3,2,1,0:T(8,128)} %get-tuple-element.245) | copy-start | bytes 3145732 | tf_op jit(solution)/shard_map/while
  62.0 8.2 %copy-start.1 = (f32[16,4,64,64]{3,2,1,0:T(8,128)S(1)}, f32[16,4,64,64]{3,2,1,0:T(8,128)}, u32[]{:S(2)}) copy-start(f32[16,4,64,64]{3,2,1,0:T(8,128)} %get-tuple-element.245) | copy-start | bytes 3145732 | tf_op jit(solution)/shard_map/while
  75.1 8.2 %copy-start.1 = (f32[16,4,64,64]{3,2,1,0:T(8,128)S(1)}, f32[16,4,64,64]{3,2,1,0:T(8,128)}, u32[]{:S(2)}) copy-start(f32[16,4,64,64]{3,2,1,0:T(8,128)} %get-tuple-element.245) | copy-start | bytes 3145732 | tf_op jit(solution)/shard_map/while
  88.3 8.2 %copy-start.1 = (f32[16,4,64,64]{3,2,1,0:T(8,128)S(1)}, f32[16,4,64,64]{3,2,1,0:T(8,128)}, u32[]{:S(2)}) copy-start(f32[16,4,64,64]{3,2,1,0:T(8,128)} %get-tuple-element.245) | copy-start | bytes 3145732 | tf_op jit(solution)/shard_map/while
  101.5 8.2 %copy-start.1 = (f32[16,4,64,64]{3,2,1,0:T(8,128)S(1)}, f32[16,4,64,64]{3,2,1,0:T(8,128)}, u32[]{:S(2)}) copy-start(f32[16,4,64,64]{3,2,1,0:T(8,128)} %get-tuple-element.245) | copy-start | bytes 3145732 | tf_op jit(solution)/shard_map/while
  114.7 8.2 %copy-start.1 = (f32[16,4,64,64]{3,2,1,0:T(8,128)S(1)}, f32[16,4,64,64]{3,2,1,0:T(8,128)}, u32[]{:S(2)}) copy-start(f32[16,4,64,64]{3,2,1,0:T(8,128)} %get-tuple-element.245) | copy-start | bytes 3145732 | tf_op jit(solution)/shard_map/while
  140.7 40.0 %all-to-all-start = ((f32[16,128,256]{2,1,0:T(8,128)}), f32[16,128,256]{2,1,0:T(8,128)}, u32[]{:S(2)}, u32[]{:S(2)}) async-start(f32[16,128,256]{2,1,0:T(8,128)} %bitcast.116), calls=%async_computation | async-start | bytes 4194304 | tf_op jit(solution)/shard_map/all_to_all | solution.py:32
  182.5 80.7 %copy-start.9 = (s32[16,8]{0,1:T(8,128)S(1)}, s32[16,8]{0,1:T(8,128)}, u32[]{:S(2)}) copy-start(s32[16,8]{0,1:T(8,128)} %param.30) | copy-start | bytes 1540
  216.8 15.4 %collective-permute-start = (bf16[128,4096]{0,1:T(8,128)(2,1)S(1)}, bf16[128,4096]{0,1:T(8,128)(2,1)S(1)}, u32[]{:S(2)}, u32[]{:S(2)}) collective-permute-start(bf16[128,4096]{0,1:T(8,128)(2,1)S(1)} %bitcast.111), channel_id=1, source_target_pairs={{0,1},{1,2},{2,3},{3,4},{4,5},{5,6},{6,7},{7,0},{8,9},{9,10},{10,1... | collective-permute-start | bytes 3145736 | tf_op jit(solution)/shard_map/ppermute | solution.py:18
  232.2 15.5 %copy-start.4 = (bf16[128,4096]{0,1:T(8,128)(2,1)}, bf16[128,4096]{0,1:T(8,128)(2,1)S(1)}, u32[]{:S(2)}) copy-start(bf16[128,4096]{0,1:T(8,128)(2,1)S(1)} %collective-permute-done) | copy-start | bytes 3145732
  232.2 15.4 %collective-permute-start.1 = (bf16[128,4096]{0,1:T(8,128)(2,1)S(1)}, bf16[128,4096]{0,1:T(8,128)(2,1)S(1)}, u32[]{:S(2)}, u32[]{:S(2)}) collective-permute-start(bf16[128,4096]{0,1:T(8,128)(2,1)S(1)} %collective-permute-done), channel_id=1, source_target_pairs={{0,1},{1,2},{2,3},{3,4},{4,5},{5,6},{6,7},{7,0},{8,9},{9,10},{10,1... | collective-permute-start | bytes 3145736 | tf_op jit(solution)/shard_map/ppermute | solution.py:18
  232.3 15.4 %collective-permute-start.4 = (bf16[128,4096]{0,1:T(8,128)(2,1)S(1)}, bf16[128,4096]{0,1:T(8,128)(2,1)}, u32[]{:S(2)}, u32[]{:S(2)}) collective-permute-start(bf16[128,4096]{0,1:T(8,128)(2,1)S(1)} %bitcast.112), channel_id=1, source_target_pairs={{0,7},{1,0},{2,1},{3,2},{4,3},{5,4},{6,5},{7,6},{8,15},{9,8},{10,9... | collective-permute-start | bytes 3145736 | tf_op jit(solution)/shard_map/ppermute | solution.py:20
  247.7 15.5 %collective-permute-start.2 = (bf16[128,4096]{0,1:T(8,128)(2,1)S(1)}, bf16[128,4096]{0,1:T(8,128)(2,1)}, u32[]{:S(2)}, u32[]{:S(2)}) collective-permute-start(bf16[128,4096]{0,1:T(8,128)(2,1)S(1)} %collective-permute-done.1), channel_id=1, source_target_pairs={{0,1},{1,2},{2,3},{3,4},{4,5},{5,6},{6,7},{7,0},{8,9},{9,10},{10,1... | collective-permute-start | bytes 3145736 | tf_op jit(solution)/shard_map/ppermute | solution.py:18
  247.7 37.2 %collective-permute-start.5 = (bf16[128,4096]{0,1:T(8,128)(2,1)}, bf16[128,4096]{0,1:T(8,128)(2,1)}, u32[]{:S(2)}, u32[]{:S(2)}) collective-permute-start(bf16[128,4096]{0,1:T(8,128)(2,1)} %collective-permute-done.4), channel_id=1, source_target_pairs={{0,7},{1,0},{2,1},{3,2},{4,3},{5,4},{6,5},{7,6},{8,15},{9,8},{10,9... | collective-permute-start | bytes 3145736 | tf_op jit(solution)/shard_map/ppermute | solution.py:20
  263.2 22.6 %collective-permute-start.3 = (bf16[128,4096]{0,1:T(8,128)(2,1)}, bf16[128,4096]{0,1:T(8,128)(2,1)}, u32[]{:S(2)}, u32[]{:S(2)}) collective-permute-start(bf16[128,4096]{0,1:T(8,128)(2,1)} %collective-permute-done.2), channel_id=1, source_target_pairs={{0,1},{1,2},{2,3},{3,4},{4,5},{5,6},{6,7},{7,0},{8,9},{9,10},{10,1... | collective-permute-start | bytes 3145736 | tf_op jit(solution)/shard_map/ppermute | solution.py:18
  284.9 13.5 %collective-permute-start.6 = (bf16[128,4096]{0,1:T(8,128)(2,1)}, bf16[128,4096]{0,1:T(8,128)(2,1)S(1)}, u32[]{:S(2)}, u32[]{:S(2)}) collective-permute-start(bf16[128,4096]{0,1:T(8,128)(2,1)} %collective-permute-done.5), channel_id=1, source_target_pairs={{0,7},{1,0},{2,1},{3,2},{4,3},{5,4},{6,5},{7,6},{8,15},{9,8},{10,9... | collective-permute-start | bytes 3145736 | tf_op jit(solution)/shard_map/ppermute | solution.py:20
  311.5 16.4 %copy-start.10 = (s32[16,8]{0,1:T(8,128)S(1)}, s32[16,8]{0,1:T(8,128)}, u32[]{:S(2)}) copy-start(s32[16,8]{0,1:T(8,128)} %param.31) | copy-start | bytes 1540
  312.8 10.4 %all-to-all-start.2 = ((f32[8,3,1024]{2,1,0:T(4,128)}), f32[8,3,1024]{2,1,0:T(4,128)S(1)}, u32[]{:S(2)}, u32[]{:S(2)}) async-start(f32[8,3,1024]{2,1,0:T(4,128)} %broadcast_in_dim.23), calls=%async_computation.2 | async-start | bytes 262144 | tf_op jit(solution)/shard_map/all_to_all | solution.py:50
  324.4 11.0 %all-to-all-start.3 = ((f32[16,3,128]{2,1,0:T(4,128)}), f32[16,3,128]{2,1,0:T(4,128)S(1)}, u32[]{:S(2)}, u32[]{:S(2)}) async-start(f32[16,3,128]{2,1,0:T(4,128)} %broadcast_in_dim.25), calls=%async_computation.3 | async-start | bytes 65536 | tf_op jit(solution)/shard_map/all_to_all | solution.py:50
  (14 other events, 48.9 us)
